TPU v7x, 32 devices: a whole 2x2x4 slice. The times are simulated.
32 devices in a mesh: fsdp: 8 (over z, core), tp: 4 (over y, x).
Axes of the slice: x: 2, y: 2, z: 4, core: 2. Of those that a mesh axis runs over, the one named last changes fastest.
Arguments:
- hidden: bfloat16 [3072, 7168], P('fsdp'), may hold values from -72 to 72
- w_query: bfloat16 [7168, 4096], P('fsdp', 'tp'), may hold values from -0.0625 to 0.0625
- w_key: bfloat16 [7168, 1024], P('fsdp', 'tp'), may hold values from -0.0625 to 0.0625
- w_value: bfloat16 [7168, 1024], P('fsdp', 'tp'), may hold values from -0.0625 to 0.0625
- w_out: bfloat16 [4096, 7168], P('tp', 'fsdp'), may hold values from -0.09375 to 0.09375
- exp_query: int32 [56, 32], replicated, may hold values from -1 to 1
- exp_key: int32 [56, 8], replicated, may hold values from -1 to 1
- exp_value: int32 [56, 8], replicated, may hold values from -1 to 1
- exp_out: int32 [32, 56], replicated, may hold values from -1 to 1
- owner: int32 [8], replicated, may hold values from 0 to 7, each once
Outputs:
- attended: bfloat16 [3072, 7168], P('fsdp', 'tp')
Inputs may be any that keep to these rules, and one draw needn't show every extreme that they name: Trainer shard i holds logical slab owner[i]; every slab is held once.
All inputs are finite; a program needn't handle non-finite values.
Results may differ from a plain program's by a relative error of at most 0.038.
Values may be sent and summed in bfloat16 or wider, within the bound.
A program may use at most 128 MiB of HBM per device.

v0:
```python
from functools import partial
import math
import jax
import jax.numpy as jnp
from jax import lax
from jax.sharding import PartitionSpec as P

HQ = 32
HK = 8
HD = 128
neg_large = -1e30


def block_factor(exponents, row_start, row_count, col_start, col_count, block_size):
    repeated = jnp.repeat(exponents, block_size, axis=0)
    picked = lax.dynamic_slice_in_dim(repeated, row_start, row_count, 0)
    repeated = jnp.repeat(picked, block_size, axis=1)
    picked = lax.dynamic_slice_in_dim(repeated, col_start, col_count, 1)
    return jnp.exp2(picked.astype(jnp.float32))


def block_update(state, query_half, pos_half, keys_part, values_part, key_pos, inv_root):
    row_max, row_sum, accum = state
    causal = pos_half[:, None] >= key_pos[None, :]
    scores = (
        jnp.einsum("tgjd,ngd->gjtn", query_half, keys_part, preferred_element_type=jnp.float32)
        * inv_root
    )
    scores = jnp.where(causal, scores, neg_large)
    new_max = jnp.maximum(row_max, jnp.max(scores, axis=3))
    rescale = jnp.exp(row_max - new_max)
    weights = jnp.where(causal, jnp.exp(scores - new_max[..., None]), 0.0)
    row_sum = row_sum * rescale + jnp.sum(weights, axis=3)
    accum = accum * rescale[..., None] + jnp.einsum(
        "gjtn,ngd->gjtd",
        weights.astype(jnp.bfloat16),
        values_part,
        preferred_element_type=jnp.float32,
    )
    return (new_max, row_sum, accum)


def keep_state(state):
    return state


def body(hidden, w_query, w_key, w_value, w_out, exp_query, exp_key, exp_value, exp_out, owner):
    fsdp_index = lax.axis_index("fsdp")
    tp_index = lax.axis_index("tp")
    slab_rows = w_query.shape[0]
    groups = owner.shape[0]
    tokens = hidden.shape[0]
    model_width = hidden.shape[1]
    block_size = model_width // exp_query.shape[0]
    slab_start = owner[fsdp_index] * slab_rows
    query_cols = w_query.shape[1]
    key_cols = w_key.shape[1]

    def scaled_rows(weight, exponents):
        col_count = weight.shape[1]
        factor = block_factor(
            exponents, slab_start, slab_rows, tp_index * col_count, col_count, block_size
        )
        return (weight.astype(jnp.float32) * factor).astype(jnp.bfloat16)

    query_local = scaled_rows(w_query, exp_query)
    key_local = scaled_rows(w_key, exp_key)
    value_local = scaled_rows(w_value, exp_value)
    out_rows = w_out.shape[0]
    out_factor = block_factor(
        exp_out, tp_index * out_rows, out_rows, slab_start, slab_rows, block_size
    )
    out_local = (w_out.astype(jnp.float32) * out_factor).astype(jnp.bfloat16)
    arranged = jnp.take(hidden.reshape(tokens, groups, slab_rows), owner, axis=1).reshape(
        tokens, model_width
    )
    pieces = (
        lax.all_gather(query_local, "fsdp", axis=0, tiled=True),
        lax.all_gather(key_local, "fsdp", axis=0, tiled=True),
        lax.all_gather(value_local, "fsdp", axis=0, tiled=True),
    )
    query_sum, key_sum, value_sum = tuple(
        (jnp.dot(arranged, weight, preferred_element_type=jnp.float32) for weight in pieces)
    )
    query = query_sum.astype(jnp.bfloat16)
    key_here = key_sum.astype(jnp.bfloat16)
    value_here = value_sum.astype(jnp.bfloat16)
    half_rows = tokens // 2
    local_pos = fsdp_index * tokens + jnp.arange(tokens, dtype=jnp.int32)
    group_size = HQ // HK
    kv_heads = key_cols // HD
    query_halves = query.reshape(2, half_rows, kv_heads, group_size, HD)
    pos_halves = local_pos.reshape(2, half_rows)
    pos_top = jnp.max(pos_halves, axis=1)
    inv_root = 1.0 / math.sqrt(HD)
    one_state = (
        jnp.full((kv_heads, group_size, half_rows), neg_large, jnp.float32),
        jnp.zeros((kv_heads, group_size, half_rows), jnp.float32),
        jnp.zeros((kv_heads, group_size, half_rows, HD), jnp.float32),
    )
    offset = jnp.int32(0)
    key_piece = lax.all_gather(key_here, "fsdp", axis=0, tiled=True)
    value_piece = lax.all_gather(value_here, "fsdp", axis=0, tiled=True)
    states = list((one_state, one_state))
    piece_rows = key_piece.shape[0]
    for block_low in range(0, piece_rows, 1024):
        block_high = min(block_low + 1024, piece_rows)
        width_here = block_high - block_low
        keys_part = key_piece[block_low:block_high].reshape(width_here, kv_heads, HD)
        values_part = value_piece[block_low:block_high].reshape(width_here, kv_heads, HD)
        key_pos = offset + block_low + jnp.arange(width_here, dtype=jnp.int32)
        for attend_which in range(2):
            update = partial(
                block_update,
                query_half=query_halves[attend_which],
                pos_half=pos_halves[attend_which],
                keys_part=keys_part,
                values_part=values_part,
                key_pos=key_pos,
                inv_root=inv_root,
            )
            states[attend_which] = lax.cond(
                offset + block_low <= pos_top[attend_which],
                update,
                keep_state,
                states[attend_which],
            )
    final_states = tuple(states)
    context_parts = []
    for which in range(2):
        row_max, row_sum, accum = final_states[which]
        part_context = (accum / row_sum[..., None]).astype(jnp.bfloat16)
        context_parts.append(part_context.transpose(2, 0, 1, 3).reshape(half_rows, query_cols))
    context = jnp.concatenate(context_parts, axis=0)
    column_terms = jnp.dot(
        context,
        lax.all_gather(out_local, "fsdp", axis=1, tiled=True),
        preferred_element_type=jnp.float32,
    )
    slab_ids = jnp.arange(groups, dtype=jnp.int32)
    inverse = jnp.sum(
        slab_ids[:, None] * (owner[:, None] == slab_ids[None, :]).astype(jnp.int32), axis=0
    )
    ordered = jnp.take(column_terms.reshape(tokens, groups, slab_rows), inverse, axis=1).reshape(
        tokens, model_width
    )
    result = lax.psum_scatter(ordered.astype(jnp.bfloat16), "tp", scatter_dimension=1, tiled=True)
    return result


def solution(mesh):
    placed = (
        P("fsdp", None),
        P("fsdp", "tp"),
        P("fsdp", "tp"),
        P("fsdp", "tp"),
        P("tp", "fsdp"),
        P(),
        P(),
        P(),
        P(),
        P(),
    )
    return jax.shard_map(
        body, mesh=mesh, in_specs=placed, out_specs=P("fsdp", "tp"), check_vma=False
    )
```

profile of v0, /device:TPU:0, one launch (start us, length us, event | category | flops | bytes accessed | tf_op | source)
XLA Modules:
  0.0 532.7 jit_solution(14240318342266903279)
XLA Ops:
  6.5 1.2 dynamic_slice.27
  8.4 0.8 copy.90
  10.6 1.0 broadcast_in_dim.180
  11.6 2.7 copy.224
  14.2 2.1 multiply_convert_fusion.3
  16.5 1.0 broadcast_in_dim.184
  17.5 0.9 copy.223
  18.4 1.0 multiply_convert_fusion.2
  19.4 8.3 %copy.85 = bf16[384,7168]{0,1:T(8,128)(2,1)} copy(bf16[384,7168]{1,0:T(8,128)(2,1)} %param.22) | data formatting | bytes 11010048 | tf_op args[0]
  27.7 8.1 %copy.86 = bf16[384,8,896]{2,0,1:T(8,128)(2,1)} copy(bf16[384,8,896]{0,2,1:T(8,128)(2,1)} %bitcast.184) | data formatting | bytes 11010048 | tf_op jit(solution)/shard_map/reshape | solution.py:74
  35.8 6.3 %gather_fusion = bf16[8,384,896]{2,1,0:T(8,128)(2,1)} fusion(bf16[384,8,896]{2,0,1:T(8,128)(2,1)} %copy.86, s32[1024]{0:T(1024)S(1)} %pad_clamp_fusion.1), kind=kCustom, calls=%fused_computation | custom fusion | bytes 11010080 | tf_op jit(solution)/shard_map/jit(_take)/gather | solution.py:74
  42.1 8.4 %copy.87 = bf16[384,8,896]{0,2,1:T(8,128)(2,1)} copy(bf16[384,8,896]{2,0,1:T(8,128)(2,1)} %bitcast.181) | data formatting | bytes 11010048 | tf_op jit(solution)/shard_map/jit(_take)/gather | solution.py:74
  50.7 7.3 %bitcast_select_fusion.7 = bf16[384,7168]{0,1:T(8,128)(2,1)} fusion(bf16[384,8,896]{0,2,1:T(8,128)(2,1)} %copy.87, pred[7168]{0:T(1024)(128)(4,1)S(1)} %broadcast_in_dim.175), kind=kLoop, calls=%fused_computation.117 | loop fusion | flops 2752512 | bytes 11017216 | tf_op jit(solution)/shard_map/jit(_take)/select_n | solution.py:74
  58.1 3.8 all-gather.7.cloned.1.call-done
  61.8 6.0 %convolution_convert_fusion.2 = bf16[384,256]{1,0:T(8,128)(2,1)} fusion(bf16[384,7168]{0,1:T(8,128)(2,1)} %bitcast_select_fusion.7, bf16[7168,256]{1,0:T(8,128)(2,1)} %all-gather.7.cloned.1.call-done), kind=kOutput, calls=%fused_computation.124 | convolution fusion | flops 1409384448 | bytes 9371648 | tf_op jit(solution)/shard_map/dot_general | solution.py:83
  67.9 37.0 %all-gather.13.cloned.1.call-done = bf16[7168,256]{1,0:T(8,128)(2,1)} async-done(((bf16[896,256]{1,0:T(8,128)(2,1)}), bf16[7168,256]{1,0:T(8,128)(2,1)}) %all-gather.13.cloned.1.call-update) | async-done | bytes 3670032 | tf_op jit(solution)/shard_map/all_gather | solution.py:80
  104.8 6.0 %convolution_convert_fusion.1 = bf16[384,256]{1,0:T(8,128)(2,1)} fusion(bf16[384,7168]{0,1:T(8,128)(2,1)} %bitcast_select_fusion.7, bf16[7168,256]{1,0:T(8,128)(2,1)} %all-gather.13.cloned.1.call-done), kind=kOutput, calls=%fused_computation.123 | convolution fusion | flops 1409384448 | bytes 9371648 | tf_op jit(solution)/shard_map/dot_general | solution.py:83
  111.3 6.4 %broadcast_in_dim.182 = s32[896,32,128]{2,1,0:T(8,128)} broadcast(s32[896,32]{1,0:T(8,128)S(1)} %constant_dynamic-slice_fusion.2), dimensions={0,1} | broadcast | bytes 14794752 | tf_op jit(solution)/shard_map/broadcast_in_dim | solution.py:17
  117.7 25.4 %copy.221 = s32[112,8,32,128]{3,1,2,0:T(8,128)} copy(s32[112,8,32,128]{3,2,1,0:T(8,128)} %bitcast.178) | data formatting | bytes 29360128
  143.1 4.1 multiply_convert_fusion.1
  147.5 8.0 %broadcast_in_dim.186 = s32[1024,56,128]{2,1,0:T(8,128)S(1)} broadcast(s32[1024,56]{1,0:T(8,128)S(1)} %constant_dynamic-slice_fusion), dimensions={0,1} | broadcast | bytes 29589504 | tf_op jit(solution)/shard_map/broadcast_in_dim | solution.py:17
  155.6 13.7 %copy.220 = s32[128,8,56,128]{3,1,2,0:T(8,128)} copy(s32[128,8,56,128]{3,2,1,0:T(8,128)S(1)} %bitcast.177) | data formatting | bytes 58720256
  169.3 4.2 multiply_convert_fusion
  180.2 1.5 fusion.108
  181.7 0.9 reshape.158
  182.6 1.5 fusion.107
  184.1 0.9 reshape.163
  185.1 0.9 reshape.165
  186.3 104.8 %all-gather.11.cloned.1.call-done = bf16[7168,1024]{1,0:T(8,128)(2,1)} async-done(((bf16[896,1024]{1,0:T(8,128)(2,1)}), bf16[7168,1024]{1,0:T(8,128)(2,1)}) %all-gather.11.cloned.1.call-update) | async-done | bytes 14680080 | tf_op jit(solution)/shard_map/all_gather | solution.py:78
  291.1 10.7 %convolution_convert_fusion = bf16[384,1024]{1,0:T(8,128)(2,1)S(1)} fusion(bf16[384,7168]{0,1:T(8,128)(2,1)} %bitcast_select_fusion.7, bf16[7168,1024]{1,0:T(8,128)(2,1)} %all-gather.11.cloned.1.call-done), kind=kOutput, calls=%fused_computation.122 | convolution fusion | flops 5637537792 | bytes 20971520 | tf_op jit(solution)/shard_map/dot_general | solution.py:83
  302.2 9.8 %conditional.9 = (f32[2,4,192]{2,1,0:T(4,128)}, f32[2,4,192]{2,1,0:T(4,128)S(1)}, f32[2,4,192,128]{3,2,1,0:T(8,128)S(1)}) conditional(s32[]{:T(128)} %bitcast.38, () %tuple.52, (s32[1,192]{1,0:T(1,128)S(1)}, s32[1024]{0:T(1024)S(1)}, bf16[1024,2,128]{2,1,0:T(2,128)(2,1)}, bf16[192,2,4,128]{3,2,1,0:T(4,128)(2,1)S(1)}, ...), branch_computations={%region_14.15_spmd, %region_15.18_spmd} | conditional | flops 826152960 | bytes 24058676 | solution.py:122
  302.4 2.5 fusion.49
  305.5 2.8 fusion.51
  309.0 2.7 fusion.55
  312.9 1.0 squeeze.4
  313.9 15.2 %conditional.6 = (f32[2,4,192]{2,1,0:T(4,128)}, f32[2,4,192]{2,1,0:T(4,128)S(1)}, f32[2,4,192,128]{3,2,1,0:T(8,128)S(1)}) conditional(s32[]{:T(128)} %bitcast.26, () %tuple.47, (s32[1,192]{1,0:T(1,128)}, s32[1024]{0:T(1024)S(1)}, bf16[1024,2,128]{2,1,0:T(2,128)(2,1)}, bf16[192,2,4,128]{3,2,1,0:T(4,128)(2,1)}, bf16[1024,2,128]{2,1,0:T(2,128)(2,1)}) %tuple.147), branch_computations={%region_2.3_spmd, %region_3.6_spmd} | conditional | flops 826152960 | bytes 24058676 | solution.py:122
  318.8 0.9 broadcast_compare_fusion
  319.7 2.6 fusion
  322.9 2.8 fusion.2
  326.4 2.7 fusion.6
  330.8 93.8 %all-gather.17.cloned.1.call-done = bf16[1024,7168]{1,0:T(8,128)(2,1)} async-done(((bf16[1024,896]{1,0:T(8,128)(2,1)}), bf16[1024,7168]{1,0:T(8,128)(2,1)}) %all-gather.17.cloned.1.call-update) | async-done | bytes 14680080 | tf_op jit(solution)/shard_map/all_gather | solution.py:137
  424.6 11.6 %fusion.99 = bf16[384,7168]{1,0:T(8,128)(2,1)S(1)} fusion(bf16[1024,7168]{1,0:T(8,128)(2,1)} %all-gather.17.cloned.1.call-done, bf16[192,1024]{1,0:T(8,128)(2,1)S(1)} %reshape.169, bf16[192,1024]{1,0:T(8,128)(2,1)S(1)} %reshape.168), kind=kOutput, calls=%fused_computation.127 | convolution fusion | flops 5638717440 | bytes 20971520 | tf_op jit(solution)/shard_map/dot_general | solution.py:135
  436.2 3.2 copy.222
  439.5 6.3 %gather_fusion.1 = bf16[8,384,896]{2,1,0:T(8,128)(2,1)} fusion(bf16[384,8,896]{2,0,1:T(8,128)(2,1)} %bitcast.182, s32[1024]{0:T(1024)} %pad_clamp_fusion), kind=kCustom, calls=%fused_computation.1 | custom fusion | bytes 11010080 | tf_op jit(solution)/shard_map/jit(_take)/gather | solution.py:144
  445.7 8.3 %copy.112 = bf16[384,8,896]{0,2,1:T(8,128)(2,1)} copy(bf16[384,8,896]{2,0,1:T(8,128)(2,1)} %bitcast.183) | data formatting | bytes 11010048 | tf_op jit(solution)/shard_map/jit(_take)/gather | solution.py:144
  454.0 7.3 %fusion.98 = bf16[384,7168]{0,1:T(8,128)(2,1)} fusion(bf16[384,8,896]{0,2,1:T(8,128)(2,1)} %copy.112, pred[7168]{0:T(1024)(128)(4,1)S(1)} %copy-done.14), kind=kLoop, calls=%fused_computation.116 | loop fusion | flops 2752512 | bytes 11017216 | tf_op jit(solution)/shard_map/convert_element_type | solution.py:147
  461.4 61.8 %reduce-scatter.2.cloned.1.call-done = bf16[384,1792]{0,1:T(8,128)(2,1)} async-done(((bf16[384,7168]{0,1:T(8,128)(2,1)}), bf16[384,1792]{0,1:T(8,128)(2,1)}) %reduce-scatter.2.cloned.1.call-update) | async-done | bytes 1376272 | tf_op jit(solution)/shard_map/reduce_scatter | solution.py:147
  523.2 2.5 copy.113
  (95 shorter events, 11.2 us)
Async XLA Ops:
  6.5 140.8 %copy-start = (s32[32,56]{1,0:T(8,128)S(1)}, s32[32,56]{1,0:T(8,128)}, u32[]{:S(2)}) copy-start(s32[32,56]{1,0:T(8,128)} %param.30) | copy-start | bytes 21508
  6.5 55.3 %all-gather.7.cloned.1.call-start = ((), (), s32[]{:S(2)}) async-start(), calls=%async_computation.1 | async-start | bytes 4128768 | tf_op jit(solution)/shard_map/all_gather | solution.py:79
  10.5 3.8 copy-start.8
  16.4 2.0 copy-start.9
  16.4 88.4 %all-gather.13.cloned.1.call-start = ((), (), s32[]{:S(2)}) async-start(), calls=%async_computation.4 | async-start | bytes 4128768 | tf_op jit(solution)/shard_map/all_gather | solution.py:80
  19.4 160.9 %all-gather.9.cloned.1.call-start = ((), (), s32[]{:S(2)}) async-start(), calls=%async_computation.2 | async-start | bytes 1769472 | tf_op jit(solution)/shard_map/all_gather | solution.py:102
  27.7 8.1 %copy-start.16 = (s32[8]{0:T(128)S(1)}, s32[8]{0:T(128)}, u32[]{:S(2)}) copy-start(s32[8]{0:T(128)} %param.31) | copy-start | bytes 100
  67.8 43.1 %copy-start.15 = (s32[56,32]{0,1:T(8,128)S(1)}, s32[56,32]{0,1:T(8,128)}, u32[]{:S(2)}) copy-start(s32[56,32]{0,1:T(8,128)} %param.27) | copy-start | bytes 21508
  67.8 114.8 %all-gather.15.cloned.1.call-start = ((), (), s32[]{:S(2)}) async-start(), calls=%async_computation.5 | async-start | bytes 1769472 | tf_op jit(solution)/shard_map/all_gather | solution.py:103
  110.9 180.2 %all-gather.11.cloned.1.call-start = ((), (), s32[]{:S(2)}) async-start(), calls=%async_computation.3 | async-start | bytes 16515072 | tf_op jit(solution)/shard_map/all_gather | solution.py:78
  117.7 25.4 %copy-start.2 = (bf16[896,1024]{1,0:T(8,128)(2,1)S(1)}, bf16[896,1024]{1,0:T(8,128)(2,1)}, u32[]{:S(2)}) copy-start(bf16[896,1024]{1,0:T(8,128)(2,1)} %param.23) | copy-start | bytes 5505028
  147.3 277.4 %all-gather.17.cloned.1.call-start = ((), (), s32[]{:S(2)}) async-start(), calls=%async_computation.6 | async-start | bytes 16515072 | tf_op jit(solution)/shard_map/all_gather | solution.py:137
  155.6 13.7 %copy-start.3 = (bf16[1024,896]{1,0:T(8,128)(2,1)S(1)}, bf16[1024,896]{1,0:T(8,128)(2,1)}, u32[]{:S(2)}) copy-start(bf16[1024,896]{1,0:T(8,128)(2,1)} %param.26) | copy-start | bytes 5505028
  173.5 349.7 %reduce-scatter.2.cloned.1.call-start = ((), (), s32[]{:S(2)}) async-start(), calls=%async_computation.7 | async-start | bytes 6881280 | tf_op jit(solution)/shard_map/reduce_scatter | solution.py:147
  179.0 132.9 %copy-start.12 = (s32[1024]{0:T(1024)}, s32[1024]{0:T(1024)S(1)}, u32[]{:S(2)}) copy-start(s32[1024]{0:T(1024)S(1)} %iota_add_fusion.1) | copy-start | bytes 12292
  179.0 132.9 %copy-start.10 = (s32[1024]{0:T(1024)}, s32[1024]{0:T(1024)S(1)}, u32[]{:S(2)}) copy-start(s32[1024]{0:T(1024)S(1)} %iota_add_fusion) | copy-start | bytes 12292
  302.4 6.6 %copy-start.6 = (bf16[1024,2,128]{2,1,0:T(2,128)(2,1)S(1)}, bf16[1024,2,128]{2,1,0:T(2,128)(2,1)}, u32[]{:S(2)}) copy-start(bf16[1024,2,128]{2,1,0:T(2,128)(2,1)} %get-tuple-element.334) | copy-start | bytes 1572868 | tf_op jit(solution)/shard_map/cond
  313.9 15.2 %copy-start.4 = (bf16[1024,2,128]{2,1,0:T(2,128)(2,1)S(1)}, bf16[1024,2,128]{2,1,0:T(2,128)(2,1)}, u32[]{:S(2)}) copy-start(bf16[1024,2,128]{2,1,0:T(2,128)(2,1)} %reshape.165) | copy-start | bytes 1572868
  313.9 15.2 %copy-start.13 = (s32[1024]{0:T(1024)S(1)}, s32[1024]{0:T(1024)}, u32[]{:S(2)}) copy-start(s32[1024]{0:T(1024)} %copy-done.12) | copy-start | bytes 12292
  319.7 6.7 %copy-start.7 = (bf16[1024,2,128]{2,1,0:T(2,128)(2,1)S(1)}, bf16[1024,2,128]{2,1,0:T(2,128)(2,1)}, u32[]{:S(2)}) copy-start(bf16[1024,2,128]{2,1,0:T(2,128)(2,1)} %get-tuple-element.313) | copy-start | bytes 1572868 | tf_op jit(solution)/shard_map/cond
  329.1 0.7 copy-start.11
  445.7 8.3 %copy-start.14 = (pred[7168]{0:T(1024)(128)(4,1)S(1)}, pred[7168]{0:T(1024)(128)(4,1)}, u32[]{:S(2)}) copy-start(pred[7168]{0:T(1024)(128)(4,1)} %broadcast_in_dim.172) | copy-start | bytes 21508
  454.0 71.7 %copy-start.1 = (s32[32,56]{1,0:T(8,128)S(1)}, s32[32,56]{1,0:T(8,128)}, u32[]{:S(2)}) copy-start(s32[32,56]{1,0:T(8,128)} %param.30) | copy-start | bytes 21508
Sparse Core Ops, SparseCore 0:
  16.5 45.2 all-gather.6
  63.5 41.3 all-gather.12
  106.5 24.0 all-gather.8
  132.1 24.3 all-gather.14
  158.0 133.0 all-gather.10
  292.5 132.0 all-gather.16
  461.5 61.6 reduce-scatter.1
where the time goes:
time: 543 us; the launch traced here: 533 us
  waiting for transfers between devices  301 us (55%)
  local copies, waits for them, and re-layouts  126 us (23%)
  matrix products  44.8 us (8%)
  other arithmetic  36.7 us (7%)
  between operations  18.7 us (3%)
    all_gather x1, waiting for transfers between devices, body(): lax.all_gather(query_local, 'fsdp', axis=0, tiled=True)  105 us
    all_gather x1, waiting for transfers between devices, body(): lax.all_gather(out_local, 'fsdp', axis=1, tiled=True)  93.8 us
    reduce_scatter x1, waiting for transfers between devices, body(): lax.psum_scatter(ordered.astype(jnp.bfloat16), 'tp', scatter_dimension=1,...  61.8 us
    unnamed x36, local copies, waits for them, and re-layouts  53.3 us
    all_gather x1, waiting for transfers between devices, body(): lax.all_gather(value_local, 'fsdp', axis=0, tiled=True)  37 us
    dot_general x3, matrix products, body(): jnp.dot(arranged, weight, preferred_element_type=jnp.float32)  22.7 us
    broadcast_in_dim x4, local copies, waits for them, and re-layouts, block_factor(): repeated = jnp.repeat(picked, block_size, axis=1)  16.5 us
    gather x2, local copies, waits for them, and re-layouts, body(): jnp.take(hidden.reshape(tokens, groups, slab_rows), owner, axis=1)  14.7 us
  transfers between devices with their start and end apart: 7, of which 5 were waited for; matrix products, arithmetic and copies ran while one was open for 30% of the time, Pallas kernels for 0%

commit v1 on v0

--- a/solution.py
+++ b/solution.py
@@ -4,6 +4,7 @@
 import jax.numpy as jnp
 from jax import lax
 from jax.sharding import PartitionSpec as P
+from jax.lax import all_to_all, axis_size
 
 HQ = 32
 HK = 8
@@ -132,11 +133,13 @@
         part_context = (accum / row_sum[..., None]).astype(jnp.bfloat16)
         context_parts.append(part_context.transpose(2, 0, 1, 3).reshape(half_rows, query_cols))
     context = jnp.concatenate(context_parts, axis=0)
-    column_terms = jnp.dot(
-        context,
-        lax.all_gather(out_local, "fsdp", axis=1, tiled=True),
-        preferred_element_type=jnp.float32,
-    )
+
+    def ladders_place(local_values):
+        prior = jnp.stack([local_values for _ in range(axis_size("fsdp"))], axis=0)
+        val = all_to_all(prior, "fsdp", 0, 0)
+        return jnp.concatenate(val, axis=1)
+
+    column_terms = jnp.dot(context, ladders_place(out_local), preferred_element_type=jnp.float32)
     slab_ids = jnp.arange(groups, dtype=jnp.int32)
     inverse = jnp.sum(
         slab_ids[:, None] * (owner[:, None] == slab_ids[None, :]).astype(jnp.int32), axis=0

time: 543 us -> 728 us (1.34)
  waiting for transfers between devices: 301 us -> 468 us
  matrix products: 44.8 us -> 54.3 us
    all_to_all x0 -> x1, waiting for transfers between devices: none -> 175 us  [ladders_place(): val = all_to_all(prior, 'fsdp', 0, 0)]
    all_gather x1 -> x0, waiting for transfers between devices: 93.8 us -> none  [body(): lax.all_gather(out_local, 'fsdp', axis=1, tiled=True)]
    all_gather x1, waiting for transfers between devices: 105 us -> 190 us  [body(): lax.all_gather(query_local, 'fsdp', axis=0, tiled=True)]
    dot_general x1, matrix products: 11.6 us -> 21.1 us  [body(): jnp.dot(context, ladders_place(out_local), preferred_element_type=jnp.flo...]
  transfers between devices with their start and end apart: 7 -> 7, of which waited for: 5 -> 5; matrix products, arithmetic and copies ran while one was open for 30% -> 23% of each run, Pallas kernels for 0% -> 0%
where the time goes in v1:
time: 728 us; the launch traced here: 718 us
  waiting for transfers between devices  468 us (64%)
  local copies, waits for them, and re-layouts  131 us (18%)
  matrix products  54.3 us (7%)
  other arithmetic  35.4 us (5%)
  between operations  18.3 us (3%)
    all_gather x1, waiting for transfers between devices, body(): lax.all_gather(query_local, 'fsdp', axis=0, tiled=True)  190 us
    all_to_all x1, waiting for transfers between devices, ladders_place(): val = all_to_all(prior, 'fsdp', 0, 0)  175 us
    reduce_scatter x1, waiting for transfers between devices, body(): lax.psum_scatter(ordered.astype(jnp.bfloat16), 'tp', scatter_dimension=1,...  61.8 us
    unnamed x36, local copies, waits for them, and re-layouts  53.2 us
    all_gather x1, waiting for transfers between devices, body(): lax.all_gather(value_local, 'fsdp', axis=0, tiled=True)  37 us
    dot_general x3, matrix products, body(): jnp.dot(arranged, weight, preferred_element_type=jnp.float32)  22.7 us
    dot_general x1, matrix products, body(): jnp.dot(context, ladders_place(out_local), preferred_element_type=jnp.flo...  21.1 us
    broadcast_in_dim x4, local copies, waits for them, and re-layouts, block_factor(): repeated = jnp.repeat(picked, block_size, axis=1)  16.5 us
  transfers between devices with their start and end apart: 7, of which 5 were waited for; matrix products, arithmetic and copies ran while one was open for 23% of the time, Pallas kernels for 0%

profile of v1, /device:TPU:0, one launch (start us, length us, event | category | flops | bytes accessed | tf_op | source)
XLA Modules:
  0.0 717.9 jit_solution(16967294579019868197)
XLA Ops:
  6.5 1.2 dynamic_slice.27
  10.6 1.0 broadcast_in_dim.180
  11.6 2.7 copy.226
  14.2 2.1 multiply_convert_fusion.3
  16.4 1.0 broadcast_in_dim.184
  17.4 0.9 copy.225
  18.3 1.0 multiply_convert_fusion.2
  19.4 8.3 %copy.90 = bf16[384,7168]{0,1:T(8,128)(2,1)} copy(bf16[384,7168]{1,0:T(8,128)(2,1)} %param.22) | data formatting | bytes 11010048 | tf_op args[0]
  27.7 8.0 %copy.91 = bf16[384,8,896]{2,0,1:T(8,128)(2,1)} copy(bf16[384,8,896]{0,2,1:T(8,128)(2,1)} %bitcast.190) | data formatting | bytes 11010048 | tf_op jit(solution)/shard_map/reshape | solution.py:75
  35.7 6.3 gather_fusion
  42.0 8.3 %copy.92 = bf16[384,8,896]{0,2,1:T(8,128)(2,1)} copy(bf16[384,8,896]{2,0,1:T(8,128)(2,1)} %bitcast.188) | data formatting | bytes 11010048 | tf_op jit(solution)/shard_map/jit(_take)/gather | solution.py:75
  50.6 7.3 %bitcast_select_fusion.7 = bf16[384,7168]{0,1:T(8,128)(2,1)} fusion(bf16[384,8,896]{0,2,1:T(8,128)(2,1)} %copy.92, pred[7168]{0:T(1024)(128)(4,1)S(1)} %broadcast_in_dim.175), kind=kLoop, calls=%fused_computation.118 | loop fusion | flops 2752512 | bytes 11017216 | tf_op jit(solution)/shard_map/jit(_take)/select_n | solution.py:75
  57.8 4.0 all-gather.6.cloned.1.call-done
  61.8 6.0 convolution_convert_fusion.2
  67.9 37.0 %all-gather.12.cloned.1.call-done = bf16[7168,256]{1,0:T(8,128)(2,1)} async-done(((bf16[896,256]{1,0:T(8,128)(2,1)}), bf16[7168,256]{1,0:T(8,128)(2,1)}) %all-gather.12.cloned.1.call-update) | async-done | bytes 3670032 | tf_op jit(solution)/shard_map/all_gather | solution.py:81
  104.8 6.0 convolution_convert_fusion.1
  111.3 6.4 broadcast_in_dim.182
  117.7 25.4 %copy.224 = s32[112,8,32,128]{3,1,2,0:T(8,128)} copy(s32[112,8,32,128]{3,2,1,0:T(8,128)} %bitcast.185) | data formatting | bytes 29360128
  143.1 4.1 multiply_convert_fusion.1
  147.5 8.0 %broadcast_in_dim.186 = s32[1024,56,128]{2,1,0:T(8,128)S(1)} broadcast(s32[1024,56]{1,0:T(8,128)S(1)} %constant_dynamic-slice_fusion), dimensions={0,1} | broadcast | bytes 29589504 | tf_op jit(solution)/shard_map/broadcast_in_dim | solution.py:18
  155.5 13.7 %copy.223 = s32[128,8,56,128]{3,1,2,0:T(8,128)} copy(s32[128,8,56,128]{3,2,1,0:T(8,128)S(1)} %bitcast.184) | data formatting | bytes 58720256
  169.2 2.9 multiply_convert_fusion
  172.2 2.5 copy.116
  174.7 6.5 stack.2
  181.2 5.6 all-to-all-start
  193.1 1.5 fusion.108
  194.6 0.9 reshape.165
  195.5 1.5 fusion.107
  196.9 0.9 reshape.170
  198.0 0.9 reshape.172
  199.2 189.8 %all-gather.10.cloned.1.call-done = bf16[7168,1024]{1,0:T(8,128)(2,1)} async-done(((bf16[896,1024]{1,0:T(8,128)(2,1)}), bf16[7168,1024]{1,0:T(8,128)(2,1)}) %all-gather.10.cloned.1.call-update) | async-done | bytes 14680080 | tf_op jit(solution)/shard_map/all_gather | solution.py:79
  388.9 10.7 %convolution_convert_fusion = bf16[384,1024]{1,0:T(8,128)(2,1)S(1)} fusion(bf16[384,7168]{0,1:T(8,128)(2,1)} %bitcast_select_fusion.7, bf16[7168,1024]{1,0:T(8,128)(2,1)} %all-gather.10.cloned.1.call-done), kind=kOutput, calls=%fused_computation.123 | convolution fusion | flops 5637537792 | bytes 20971520 | tf_op jit(solution)/shard_map/dot_general | solution.py:84
  400.0 9.7 %conditional.9 = (f32[2,4,192]{2,1,0:T(4,128)}, f32[2,4,192]{2,1,0:T(4,128)S(1)}, f32[2,4,192,128]{3,2,1,0:T(8,128)S(1)}) conditional(s32[]{:T(128)} %bitcast.38, () %tuple.52, (s32[1,192]{1,0:T(1,128)S(1)}, s32[1024]{0:T(1024)S(1)}, bf16[1024,2,128]{2,1,0:T(2,128)(2,1)}, bf16[192,2,4,128]{3,2,1,0:T(4,128)(2,1)S(1)}, ...), branch_computations={%region_14.15_spmd, %region_15.18_spmd} | conditional | flops 826152960 | bytes 24058676 | solution.py:123
  400.2 2.5 fusion.49
  403.3 2.8 fusion.51
  406.8 2.7 fusion.55
  410.7 1.1 squeeze.4
  411.7 15.1 %conditional.6 = (f32[2,4,192]{2,1,0:T(4,128)}, f32[2,4,192]{2,1,0:T(4,128)S(1)}, f32[2,4,192,128]{3,2,1,0:T(8,128)S(1)}) conditional(s32[]{:T(128)} %bitcast.26, () %tuple.47, (s32[1,192]{1,0:T(1,128)}, s32[1024]{0:T(1024)S(1)}, bf16[1024,2,128]{2,1,0:T(2,128)(2,1)}, bf16[192,2,4,128]{3,2,1,0:T(4,128)(2,1)}, bf16[1024,2,128]{2,1,0:T(2,128)(2,1)}) %tuple.145), branch_computations={%region_2.3_spmd, %region_3.6_spmd} | conditional | flops 826152960 | bytes 24058676 | solution.py:123
  417.5 2.6 fusion
  420.7 2.8 fusion.2
  424.2 2.7 fusion.6
  428.6 175.0 %all-to-all-done = bf16[8,1024,896]{1,2,0:T(8,128)(2,1)} async-done(((bf16[8,1024,896]{1,2,0:T(8,128)(2,1)}), bf16[8,1024,896]{1,2,0:T(8,128)(2,1)}, u32[]{:S(2)}, u32[]{:S(2)}) %all-to-all-start) | async-done | bytes 14680096 | tf_op jit(solution)/shard_map/all_to_all | solution.py:139
  603.6 21.1 %fusion.98 = bf16[384,8,896]{2,0,1:T(8,128)(2,1)} fusion(bf16[8,1024,896]{1,2,0:T(8,128)(2,1)} %all-to-all-done, bf16[192,1024]{1,0:T(8,128)(2,1)S(1)} %reshape.176, bf16[192,1024]{1,0:T(8,128)(2,1)S(1)} %reshape.175), kind=kOutput, calls=%fused_computation.114 | convolution fusion | flops 5638717440 | bytes 20971520 | tf_op jit(solution)/shard_map/dot_general | solution.py:142
  624.7 6.3 gather_fusion.1
  631.0 8.3 %copy.117 = bf16[384,8,896]{0,2,1:T(8,128)(2,1)} copy(bf16[384,8,896]{2,0,1:T(8,128)(2,1)} %bitcast.189) | data formatting | bytes 11010048 | tf_op jit(solution)/shard_map/jit(_take)/gather | solution.py:147
  639.3 7.3 %fusion.100 = bf16[384,7168]{0,1:T(8,128)(2,1)} fusion(bf16[384,8,896]{0,2,1:T(8,128)(2,1)} %copy.117, pred[7168]{0:T(1024)(128)(4,1)S(1)} %copy-done.14), kind=kLoop, calls=%fused_computation.117 | loop fusion | flops 2752512 | bytes 11017216 | tf_op jit(solution)/shard_map/convert_element_type | solution.py:150
  646.6 61.8 %reduce-scatter.2.cloned.1.call-done = bf16[384,1792]{0,1:T(8,128)(2,1)} async-done(((bf16[384,7168]{0,1:T(8,128)(2,1)}), bf16[384,1792]{0,1:T(8,128)(2,1)}) %reduce-scatter.2.cloned.1.call-update) | async-done | bytes 1376272 | tf_op jit(solution)/shard_map/reduce_scatter | solution.py:150
  708.4 2.5 copy.118
  (95 shorter events, 12.7 us)
Async XLA Ops:
  6.5 140.7 %copy-start = (s32[32,56]{1,0:T(8,128)S(1)}, s32[32,56]{1,0:T(8,128)}, u32[]{:S(2)}) copy-start(s32[32,56]{1,0:T(8,128)} %param.30) | copy-start | bytes 21508
  6.5 55.3 %all-gather.6.cloned.1.call-start = ((), (), s32[]{:S(2)}) async-start(), calls=%async_computation.2 | async-start | bytes 4128768 | tf_op jit(solution)/shard_map/all_gather | solution.py:80
  10.5 3.8 copy-start.8
  16.4 2.0 copy-start.9
  16.4 88.4 %all-gather.12.cloned.1.call-start = ((), (), s32[]{:S(2)}) async-start(), calls=%async_computation.5 | async-start | bytes 4128768 | tf_op jit(solution)/shard_map/all_gather | solution.py:81
  19.3 173.7 %all-gather.8.cloned.1.call-start = ((), (), s32[]{:S(2)}) async-start(), calls=%async_computation.3 | async-start | bytes 1769472 | tf_op jit(solution)/shard_map/all_gather | solution.py:103
  27.7 8.0 %copy-start.16 = (s32[8]{0:T(128)S(1)}, s32[8]{0:T(128)}, u32[]{:S(2)}) copy-start(s32[8]{0:T(128)} %param.31) | copy-start | bytes 100
  67.8 43.1 %copy-start.15 = (s32[56,32]{0,1:T(8,128)S(1)}, s32[56,32]{0,1:T(8,128)}, u32[]{:S(2)}) copy-start(s32[56,32]{0,1:T(8,128)} %param.27) | copy-start | bytes 21508
  67.8 127.6 %all-gather.14.cloned.1.call-start = ((), (), s32[]{:S(2)}) async-start(), calls=%async_computation.6 | async-start | bytes 1769472 | tf_op jit(solution)/shard_map/all_gather | solution.py:104
  110.8 278.1 %all-gather.10.cloned.1.call-start = ((), (), s32[]{:S(2)}) async-start(), calls=%async_computation.4 | async-start | bytes 16515072 | tf_op jit(solution)/shard_map/all_gather | solution.py:79
  117.7 25.4 %copy-start.2 = (bf16[896,1024]{1,0:T(8,128)(2,1)S(1)}, bf16[896,1024]{1,0:T(8,128)(2,1)}, u32[]{:S(2)}) copy-start(bf16[896,1024]{1,0:T(8,128)(2,1)} %param.23) | copy-start | bytes 5505028
  155.5 13.7 %copy-start.3 = (bf16[1024,896]{1,0:T(8,128)(2,1)S(1)}, bf16[1024,896]{1,0:T(8,128)(2,1)}, u32[]{:S(2)}) copy-start(bf16[1024,896]{1,0:T(8,128)(2,1)} %param.26) | copy-start | bytes 5505028
  181.2 422.4 %all-to-all-start = ((bf16[8,1024,896]{1,2,0:T(8,128)(2,1)}), bf16[8,1024,896]{1,2,0:T(8,128)(2,1)}, u32[]{:S(2)}, u32[]{:S(2)}) async-start(bf16[8,1024,896]{1,2,0:T(8,128)(2,1)} %stack.2), calls=%async_computation | async-start | bytes 29360128 | tf_op jit(solution)/shard_map/all_to_all | solution.py:139
  186.8 521.6 %reduce-scatter.2.cloned.1.call-start = ((), (), s32[]{:S(2)}) async-start(), calls=%async_computation.7 | async-start | bytes 6881280 | tf_op jit(solution)/shard_map/reduce_scatter | solution.py:150
  191.9 217.9 %copy-start.12 = (s32[1024]{0:T(1024)}, s32[1024]{0:T(1024)S(1)}, u32[]{:S(2)}) copy-start(s32[1024]{0:T(1024)S(1)} %iota_add_fusion.1) | copy-start | bytes 12292
  191.9 217.9 %copy-start.10 = (s32[1024]{0:T(1024)}, s32[1024]{0:T(1024)S(1)}, u32[]{:S(2)}) copy-start(s32[1024]{0:T(1024)S(1)} %iota_add_fusion) | copy-start | bytes 12292
  400.2 6.6 copy-start.6
  411.7 15.1 %copy-start.4 = (bf16[1024,2,128]{2,1,0:T(2,128)(2,1)S(1)}, bf16[1024,2,128]{2,1,0:T(2,128)(2,1)}, u32[]{:S(2)}) copy-start(bf16[1024,2,128]{2,1,0:T(2,128)(2,1)} %reshape.172) | copy-start | bytes 1572868
  411.7 15.2 %copy-start.13 = (s32[1024]{0:T(1024)S(1)}, s32[1024]{0:T(1024)}, u32[]{:S(2)}) copy-start(s32[1024]{0:T(1024)} %copy-done.12) | copy-start | bytes 12292
  417.5 6.7 copy-start.7
  426.9 0.7 copy-start.11
  631.0 8.3 %copy-start.14 = (pred[7168]{0:T(1024)(128)(4,1)S(1)}, pred[7168]{0:T(1024)(128)(4,1)}, u32[]{:S(2)}) copy-start(pred[7168]{0:T(1024)(128)(4,1)} %broadcast_in_dim.172) | copy-start | bytes 21508
  639.3 71.6 %copy-start.1 = (s32[32,56]{1,0:T(8,128)S(1)}, s32[32,56]{1,0:T(8,128)}, u32[]{:S(2)}) copy-start(s32[32,56]{1,0:T(8,128)} %param.30) | copy-start | bytes 21508
Sparse Core Ops, SparseCore 0:
  16.5 45.2 all-gather.5
  63.4 41.3 all-gather.11
  106.5 24.0 all-gather.7
  132.1 24.3 all-gather.13
  158.0 230.8 all-gather.9
  646.8 61.6 reduce-scatter.1
